TPU v7x, 256 devices: a 8x8x2 block of a 8x8x16 slice. The times are simulated.
256 devices in a mesh: groups: 2 (over z), tensor: 128 (over x, y, core).
Axes of the slice: x: 8, y: 8, z: 2, core: 2. Of those that a mesh axis runs over, the one named last changes fastest.
The devices are a block of a 8x8x16 slice.
Arguments:
- image_features: bfloat16 [256, 12800], P('groups', 'tensor'), parts along dimension 0, may hold values from -6 to 6
- image_counts: int32 [4], P('groups'), parts along dimension 0, may hold values from 1 to 64, 80 in all
- slot_position: int32 [256], P('groups'), parts along dimension 0, may hold values from 0 to 255, as said below
- text_ids: int32 [512], P('groups'), parts along dimension 0, may hold values from 0 to 49151
- norm_gain: float32 [12800], replicated, may hold values from 0.5 to 1.5
- norm_bias: float32 [12800], replicated, may hold values from -3 to 3
- proj_first: bfloat16 [6144, 12800], P('tensor'), may hold values from -0.0546875 to 0.0546875
- proj_second: bfloat16 [6144, 6144], P('tensor'), may hold values from -0.078125 to 0.078125
- embedding: bfloat16 [6144, 49152], P('tensor'), may hold values from -6 to 6
- rms_gain: float32 [6144], replicated, may hold values from 0.5 to 1.5
- gate_weight: bfloat16 [6144, 16384], P(None, 'tensor'), may hold values from -0.3125 to 0.3125
- up_weight: bfloat16 [6144, 16384], P(None, 'tensor'), may hold values from -0.3125 to 0.3125
- down_weight: bfloat16 [16384, 6144], P('tensor'), may hold values from -0.046875 to 0.046875
- output_grad: bfloat16 [512, 6144], P('groups', 'tensor'), parts along dimension 0, may hold values from -6 to 6
Outputs:
- input_grad: float32 [512, 6144], P('groups', 'tensor'), parts along dimension 0
- second_grad: float32 [12288, 6144], P(('groups', 'tensor')), parts along dimension 0
There are 2 independent parts, one for each index of `groups`. A program takes and returns all parts, laid end to end along the dimension named above; an argument that names none is the same for every part. Nothing has to cross between parts.
Inputs may be any that keep to these rules, and one draw needn't show every extreme that they name: `image_counts`: the counts sum to 80. `slot_position`: the 128 positions are distinct.
All inputs are finite; a program needn't handle non-finite values.
Results may differ from a plain program's by a relative error of at most 0.0079.
Values may be sent and summed in bfloat16 or wider, within the bound.
A program may use at most 128 MiB of HBM per device.

v0:
```python
import jax
import jax.numpy as jnp
from jax import lax
from jax.sharding import Mesh
from jax.sharding import PartitionSpec as P

LIVE = 80
TENSOR = ("tensor_0", "tensor_1", "tensor_2")
GROUPS_TENSOR = ("groups", "tensor_0", "tensor_1", "tensor_2")


def in_order(parts, dim):
    shape = list(parts.shape[1:])
    shape[dim] *= parts.shape[0]
    return jnp.moveaxis(parts, 0, dim).reshape(shape)


def all_blocks(x, axes, order):
    parts = x
    for k in order:
        parts = lax.all_gather(parts, axes[k])
    done = order[::-1]
    back = [done.index(k) for k in range(len(axes))]
    parts = parts.transpose(*back, *range(len(axes), parts.ndim))
    return parts.reshape(-1, *x.shape)


def whole_of(x, axes, order, dim):
    return in_order(all_blocks(x, axes, order), dim)


def own_block(parts, axes, order):
    inside = parts.shape[1:]
    parts = parts.reshape(*(lax.axis_size(a) for a in axes), *inside)
    parts = jnp.moveaxis(parts, order, range(len(axes))).reshape(-1, *inside)
    for k in order:
        parts = lax.psum_scatter(parts, axes[k], scatter_dimension=0, tiled=True)
    return parts[0]


def in_blocks(x, dim, size):
    before, after = (x.shape[:dim], x.shape[dim + 1 :])
    return jnp.moveaxis(x.reshape(*before, size, -1, *after), dim, 0)


def scatter_axes(x, axes, order, dim):
    size = lax.axis_size(axes)
    return own_block(in_blocks(x, dim, size), axes, order)


def one_axis_at_a_time(x, axes):
    for axis in axes:
        x = lax.psum(x, axis)
    return x


def layer_norm(rows_in, gain_in, bias_in):
    values = rows_in.astype(jnp.float32)
    centre = values - jnp.mean(values, axis=-1, keepdims=True)
    spread = jnp.mean(centre * centre, axis=-1, keepdims=True)
    return (centre * lax.rsqrt(spread + 1e-05) * gain_in + bias_in).astype(jnp.bfloat16)


def on_device(
    image_features,
    image_counts,
    slot_position,
    text_ids,
    norm_gain,
    norm_bias,
    proj_first,
    proj_second,
    embedding,
    rms_gain,
    gate_weight,
    up_weight,
    down_weight,
    output_grad,
):
    slot_total = image_features.shape[0]
    per_image = slot_total // image_counts.shape[0]
    seq_len = output_grad.shape[0]
    model_width = gate_weight.shape[0]
    col_count = output_grad.shape[1]
    slot_ids = jnp.arange(slot_total, dtype=jnp.int32)
    is_live = slot_ids % per_image < jnp.repeat(
        image_counts, per_image, total_repeat_length=slot_total
    )
    packed_order = jnp.argsort(jnp.where(is_live, 0, 1).astype(jnp.int32), stable=True)[:LIVE]
    gathered = whole_of(image_features[packed_order], TENSOR, (0, 1, 2), 1)
    positions = slot_position[packed_order]
    in_use = jnp.ones((LIVE,), dtype=bool)
    normed = layer_norm(gathered, norm_gain, norm_bias)
    hidden_pre = lax.dot_general(
        normed, proj_first, (((1,), (1,)), ((), ())), preferred_element_type=jnp.float32
    )
    act_cols = jax.nn.gelu(hidden_pre, approximate=False).astype(jnp.bfloat16)
    act_full = lax.all_gather(act_cols, TENSOR, axis=1, tiled=True)
    projected = lax.dot_general(
        act_full, proj_second, (((1,), (1,)), ((), ())), preferred_element_type=jnp.float32
    ).astype(jnp.bfloat16)
    target = jnp.where(in_use, positions, seq_len)
    text_rows = jnp.take(embedding, text_ids, axis=1).T
    tokens = text_rows.at[target].set(projected, mode="drop")
    full_tokens = lax.all_gather(tokens, TENSOR, axis=1, tiled=True)
    values = full_tokens.astype(jnp.float32)
    inverse = lax.rsqrt(jnp.mean(values * values, axis=-1, keepdims=True) + 1e-05)
    normed_tokens = (values * inverse * rms_gain).astype(jnp.bfloat16)
    gate_out = jnp.dot(normed_tokens, gate_weight, preferred_element_type=jnp.float32)
    up_out = jnp.dot(normed_tokens, up_weight, preferred_element_type=jnp.float32)
    hidden_grad = lax.dot_general(
        lax.all_gather(output_grad, TENSOR, axis=1, tiled=True),
        down_weight,
        (((1,), (1,)), ((), ())),
        preferred_element_type=jnp.float32,
    )
    sig_gate = jax.nn.sigmoid(gate_out)
    gate_grad = (hidden_grad * up_out * sig_gate * (1.0 + gate_out * (1.0 - sig_gate))).astype(
        jnp.bfloat16
    )
    up_grad = (hidden_grad * gate_out * sig_gate).astype(jnp.bfloat16)
    partial_value = lax.dot_general(
        gate_grad, gate_weight, (((1,), (1,)), ((), ())), preferred_element_type=jnp.float32
    )
    partial_value = partial_value + lax.dot_general(
        up_grad, up_weight, (((1,), (1,)), ((), ())), preferred_element_type=jnp.float32
    )
    norm_grad = scatter_axes(partial_value, TENSOR, (2, 0, 1), 1)
    offset = lax.axis_index(TENSOR) * col_count
    gain_cols = lax.dynamic_slice_in_dim(rms_gain, offset, col_count, 0)
    unit_cols = tokens.astype(jnp.float32) * inverse
    scaled = gain_cols * norm_grad
    row_sums = one_axis_at_a_time(jnp.sum(scaled * unit_cols, axis=-1), TENSOR)
    input_grad = output_grad.astype(jnp.float32) + inverse * (
        scaled - unit_cols * (row_sums / model_width)[:, None]
    )
    proj_grad = jnp.where(in_use[:, None], input_grad[positions], 0.0).astype(jnp.bfloat16)
    second_grad = lax.dot_general(
        proj_grad, act_full, (((0,), (0,)), ((), ())), preferred_element_type=jnp.float32
    )
    return (input_grad, second_grad)


def solution(mesh):
    torus = Mesh(
        mesh.devices.reshape(mesh.shape["groups"], 8, 8, 2),
        ("groups", "tensor_0", "tensor_1", "tensor_2"),
    )
    in_specs = (
        P("groups", TENSOR),
        P("groups"),
        P("groups"),
        P("groups"),
        P(),
        P(),
        P(TENSOR, None),
        P(TENSOR, None),
        P(TENSOR, None),
        P(),
        P(None, TENSOR),
        P(None, TENSOR),
        P(TENSOR, None),
        P("groups", TENSOR),
    )
    out_specs = (P("groups", TENSOR), P(GROUPS_TENSOR, None))
    return jax.shard_map(
        on_device, mesh=torus, in_specs=in_specs, out_specs=out_specs, check_vma=False
    )
```

profile of v0, /device:TPU:513, one launch (start us, length us, event | category | flops | bytes accessed | tf_op | source)
XLA Modules:
  0.0 529.5 jit_solution(11079233701716624059)
XLA Ops:
  7.2 0.0 copy-start
  7.2 0.1 all-gather.11.cloned.1.call-start
  7.3 1.4 fusion.34
  8.6 2.0 compare_select_fusion.3
  10.6 2.5 sort.17
  13.1 0.9 copy.41
  14.0 0.7 gather_fusion.2
  14.7 21.0 %all-gather = bf16[640,100]{1,0:T(8,128)(2,1)S(1)} all-gather(bf16[80,100]{1,0:T(8,128)(2,1)S(1)} %gather_fusion.2), channel_id=2, replica_groups=mesh['groups'=2,'tensor_0'=8,'tensor_1'=8,'tensor_2'=2] {'tensor_0'}, dimensions={0}, use_global_device_ids=true | all-gather | bytes 144000 | tf_op jit(solution)/shard_map/all_gather | solution.py:21
  35.7 33.0 %all-gather.1 = bf16[64,80,100]{2,1,0:T(8,128)(2,1)} all-gather(bf16[8,80,100]{2,1,0:T(8,128)(2,1)S(1)} %bitcast.49), channel_id=3, replica_groups=mesh['groups'=2,'tensor_0'=8,'tensor_1'=8,'tensor_2'=2] {'tensor_1'}, dimensions={0}, use_global_device_ids=true | all-gather | bytes 1152000 | tf_op jit(solution)/shard_map/all_gather | solution.py:21
  68.6 0.1 all-gather.11.cloned.1.call-update
  68.7 0.1 all-gather.9.cloned.1.call-start
  68.8 0.7 all-gather.9.cloned.1.call-update
  69.5 0.1 all-gather.7.cloned.1.call-start
  69.6 1.2 gather_fusion.1
  70.8 0.0 copy-start.9
  70.8 11.6 %copy.40 = bf16[48,49152]{0,1:T(8,128)(2,1)} copy(bf16[48,49152]{1,0:T(8,128)(2,1)} %param.24) | data formatting | bytes 9437184 | tf_op args[8]
  82.5 6.9 %gather_fusion = bf16[256,48]{1,0:T(8,128)(2,1)S(1)} fusion(bf16[48,49152]{0,1:T(8,128)(2,1)} %copy.40, s32[1024]{0:T(1024)S(1)} %pad_clamp_fusion.2), kind=kCustom, calls=%fused_computation | custom fusion | bytes 50176 | tf_op jit(solution)/shard_map/jit(_take)/gather | solution.py:103
  89.4 0.1 broadcast_select_fusion
  89.5 17.5 %all-gather.11.cloned.1.call-done = bf16[16,8,80,100]{3,2,1,0:T(8,128)(2,1)} async-done(((bf16[8,8,80,100]{3,2,1,0:T(8,128)(2,1)}), bf16[16,8,80,100]{3,2,1,0:T(8,128)(2,1)}) %all-gather.11.cloned.1.call-update) | async-done | bytes 2048016 | tf_op jit(solution)/shard_map/all_gather | solution.py:21
  107.0 2.3 convert_element_type.79
  109.3 0.8 copy.42
  110.1 2.3 copy-done.3
  112.4 3.9 copy.43
  116.4 6.8 %reshape.107 = f32[80,12800]{1,0:T(8,128)} reshape(f32[80,128,100]{2,1,0:T(8,128)} %copy.43) | data formatting | bytes 8192000 | tf_op jit(solution)/shard_map/convert_element_type | solution.py:58
  123.1 2.5 convert_reduce_fusion
  125.7 0.0 copy-start.11
  125.7 0.0 copy-start.12
  125.7 3.5 fusion.4
  129.3 0.1 copy-done.5
  129.4 1.0 fusion.21
  130.4 53.1 %all_gather.33 = bf16[80,6144]{0,1:T(8,128)(2,1)S(1)} all-gather(bf16[80,48]{0,1:T(8,128)(2,1)S(1)} %fusion.21), channel_id=1, replica_groups=mesh['groups'=2,'tensor_0'=8,'tensor_1'=8,'tensor_2'=2] {'tensor_0','ten..., dimensions={1}, use_global_device_ids=true | all-gather | bytes 990720 | tf_op jit(solution)/shard_map/all_gather | solution.py:98
  183.5 0.4 convolution_convert_fusion
  183.9 0.1 copy.44
  184.0 0.9 scatter_fusion
  184.9 0.7 copy.45
  185.6 0.1 all-gather.7.cloned.1.call-update
  185.7 0.3 reduce-scatter.4.cloned.1.call-start
  186.0 5.0 all-gather.9.cloned.1.call-done
  191.0 3.4 fusion.35
  194.4 77.7 %all-gather.7.cloned.1.call-done = bf16[256,6144]{0,1:T(8,128)(2,1)} async-done(((bf16[256,48]{0,1:T(8,128)(2,1)}), bf16[256,6144]{0,1:T(8,128)(2,1)}) %all-gather.7.cloned.1.call-update) | async-done | bytes 3145744 | tf_op jit(solution)/shard_map/all_gather | solution.py:105
  272.1 2.9 fusion
  275.0 3.5 fusion.10
  278.4 8.0 %fusion.9 = f32[256,6144]{1,0:T(8,128)} fusion(bf16[6144,128]{1,0:T(8,128)(2,1)} %param.26, f32[256,128]{1,0:T(8,128)S(1)} %fusion.35, bf16[6144,128]{1,0:T(8,128)(2,1)S(1)} %copy-done, bf16[256,6144]{0,1:T(8,128)(2,1)} %all-gather.7.cloned.1.call-done, f32[6144]{0:T(1024)S(1)} %copy-done.8, f32[256]{0:T(256)S(1)} %add_rsqrt_fusion, f32[256,128]{1,0:T(8,128)S(1)} %fusion.10), kind=kOutput, calls=%fused_computation.21 | convolution fusion | flops 811925504 | bytes 12870656 | tf_op jit(solution)/shard_map/dot_general | solution.py:122
  286.5 6.4 %convolution_add_fusion = f32[256,6144]{1,0:T(8,128)} fusion(f32[256,6144]{1,0:T(8,128)} %fusion.9, bf16[6144,128]{1,0:T(8,128)(2,1)S(1)} %copy-done, f32[256,128]{1,0:T(8,128)S(1)} %fusion.35, f32[256,128]{1,0:T(8,128)S(1)} %fusion.10), kind=kOutput, calls=%fused_computation.5 | convolution fusion | flops 404422656 | bytes 14417920 | tf_op jit(solution)/shard_map/dot_general | solution.py:125
  292.9 6.6 %copy.46 = f32[256,6144]{0,1:T(8,128)} copy(f32[256,6144]{1,0:T(8,128)} %convolution_add_fusion) | data formatting | bytes 12582912 | tf_op jit(solution)/shard_map/add | solution.py:125
  299.5 11.5 %copy.47 = f32[8,8,2,256,48]{4,3,1,0,2:T(8,128)} copy(f32[8,8,2,256,48]{3,4,2,1,0:T(8,128)} %bitcast.46) | data formatting | bytes 12582912 | tf_op jit(solution)/shard_map/reshape | solution.py:34
  311.0 0.1 reduce-scatter.4.cloned.1.call-update
  311.1 0.1 reduce-scatter.6.cloned.1.call-start
  311.2 30.2 %reduce-scatter.4.cloned.1.call-done = f32[64,256,48]{2,1,0:T(8,128)} async-done(((f32[128,256,48]{2,1,0:T(8,128)}), f32[64,256,48]{2,1,0:T(8,128)}) %reduce-scatter.4.cloned.1.call-update) | async-done | bytes 3145744 | tf_op jit(solution)/shard_map/reduce_scatter | solution.py:37
  341.3 0.1 reduce-scatter.6.cloned.1.call-update
  341.4 0.1 reduce-scatter.8.cloned.1.call-start
  341.5 98.7 %reduce-scatter.6.cloned.1.call-done = f32[8,256,48]{2,1,0:T(8,128)} async-done(((f32[64,256,48]{2,1,0:T(8,128)}), f32[8,256,48]{2,1,0:T(8,128)}) %reduce-scatter.6.cloned.1.call-update) | async-done | bytes 393232 | tf_op jit(solution)/shard_map/reduce_scatter | solution.py:37
  440.2 0.1 reduce-scatter.8.cloned.1.call-update
  440.2 0.1 copy.39
  440.4 0.1 dynamic_slice.3
  440.5 36.8 %reduce-scatter.8.cloned.1.call-done = f32[1,256,48]{2,1,0:T(8,128)} async-done(((f32[8,256,48]{2,1,0:T(8,128)}), f32[1,256,48]{2,1,0:T(8,128)}) %reduce-scatter.8.cloned.1.call-update) | async-done | bytes 49168 | tf_op jit(solution)/shard_map/reduce_scatter | solution.py:37
  477.3 1.1 multiply_reduce_fusion
  478.3 13.2 %psum.21 = f32[256]{0:T(256)S(1)} all-reduce(f32[256]{0:T(256)S(1)} %multiply_reduce_fusion), channel_id=1, replica_groups=mesh['groups'=2,'tensor_0'=8,'tensor_1'=8,'tensor_2'=2] {'tensor_0'}, use_global_device_ids=true, to_apply=%region_9.10 | all-reduce | flops 256 | bytes 2048 | tf_op jit(solution)/shard_map/psum | solution.py:53
  491.5 12.4 %psum.22 = f32[256]{0:T(256)S(1)} all-reduce(f32[256]{0:T(256)S(1)} %psum.21), channel_id=1, replica_groups=mesh['groups'=2,'tensor_0'=8,'tensor_1'=8,'tensor_2'=2] {'tensor_1'}, use_global_device_ids=true, to_apply=%region_10.11 | all-reduce | flops 256 | bytes 2048 | tf_op jit(solution)/shard_map/psum | solution.py:53
  503.9 14.6 %psum.23 = f32[256]{0:T(256)S(1)} all-reduce(f32[256]{0:T(256)S(1)} %psum.22), channel_id=1, replica_groups=mesh['groups'=2,'tensor_0'=8,'tensor_1'=8,'tensor_2'=2] {'tensor_2'}, use_global_device_ids=true, to_apply=%region_11.12 | all-reduce | flops 256 | bytes 2048 | tf_op jit(solution)/shard_map/psum | solution.py:53
  518.6 1.0 multiply_add_fusion
  519.6 0.7 copy.48
  520.3 0.6 gather_fusion.3
  520.9 1.7 fusion.36
  (32 shorter events, 0.1 us)
Async XLA Ops:
  7.2 271.3 %copy-start = (bf16[6144,128]{1,0:T(8,128)(2,1)S(1)}, bf16[6144,128]{1,0:T(8,128)(2,1)}, u32[]{:S(2)}) copy-start(bf16[6144,128]{1,0:T(8,128)(2,1)} %param.27) | copy-start | bytes 4718596
  7.2 62.4 %copy-start.2 = (s32[128]{0:T(128)S(1)}, s32[128]{0:T(128)}, u32[]{:S(2)}) copy-start(s32[128]{0:T(128)} %param.18) | copy-start | bytes 1540
  7.2 99.8 %all-gather.11.cloned.1.call-start = ((), (), s32[]{:S(2)}) async-start(), calls=%async_computation.8 | async-start | bytes 3932160 | tf_op jit(solution)/shard_map/all_gather | solution.py:21
  68.7 122.3 %all-gather.9.cloned.1.call-start = ((), (), s32[]{:S(2)}) async-start(), calls=%async_computation.4 | async-start | bytes 3170304 | tf_op jit(solution)/shard_map/all_gather | solution.py:112
  69.5 202.6 %all-gather.7.cloned.1.call-start = ((), (), s32[]{:S(2)}) async-start(), calls=%async_computation.3 | async-start | bytes 3170304 | tf_op jit(solution)/shard_map/all_gather | solution.py:105
  70.8 11.6 %copy-start.9 = (s32[256]{0:T(256)S(1)}, s32[256]{0:T(256)}, u32[]{:S(2)}) copy-start(s32[256]{0:T(256)} %param.19) | copy-start | bytes 3076
  110.1 2.3 copy-start.3
  123.1 6.1 %copy-start.10 = (bf16[48,12800]{1,0:T(8,128)(2,1)S(1)}, bf16[48,12800]{1,0:T(8,128)(2,1)}, u32[]{:S(2)}) copy-start(bf16[48,12800]{1,0:T(8,128)(2,1)} %param.22) | copy-start | bytes 3686404
  125.7 3.7 copy-start.5
  125.7 3.7 copy-start.11
  125.7 3.7 copy-start.12
  129.4 54.1 %copy-start.6 = (bf16[48,6144]{1,0:T(8,128)(2,1)S(1)}, bf16[48,6144]{1,0:T(8,128)(2,1)}, u32[]{:S(2)}) copy-start(bf16[48,6144]{1,0:T(8,128)(2,1)} %param.23) | copy-start | bytes 1769476
  185.6 89.3 %copy-start.8 = (f32[6144]{0:T(1024)S(1)}, f32[6144]{0:T(1024)}, u32[]{:S(2)}) copy-start(f32[6144]{0:T(1024)} %param.25) | copy-start | bytes 73732
  185.7 155.7 %reduce-scatter.4.cloned.1.call-start = ((), (), s32[]{:S(2)}) async-start(), calls=%async_computation.5 | async-start | bytes 25165824 | tf_op jit(solution)/shard_map/reduce_scatter | solution.py:37
  272.1 2.9 copy-start.4
  311.1 129.1 %reduce-scatter.6.cloned.1.call-start = ((), (), s32[]{:S(2)}) async-start(), calls=%async_computation.6 | async-start | bytes 9437184 | tf_op jit(solution)/shard_map/reduce_scatter | solution.py:37
  341.3 98.9 %copy-start.7 = (bf16[256,48]{0,1:T(8,128)(2,1)S(1)}, bf16[256,48]{0,1:T(8,128)(2,1)}, u32[]{:S(2)}) copy-start(bf16[256,48]{0,1:T(8,128)(2,1)} %param.29) | copy-start | bytes 73732
  341.4 181.2 %copy-start.1 = (bf16[6144,128]{1,0:T(8,128)(2,1)S(1)}, bf16[6144,128]{1,0:T(8,128)(2,1)}, u32[]{:S(2)}) copy-start(bf16[6144,128]{1,0:T(8,128)(2,1)} %param.27) | copy-start | bytes 4718596
  341.4 135.8 %reduce-scatter.8.cloned.1.call-start = ((), (), s32[]{:S(2)}) async-start(), calls=%async_computation.7 | async-start | bytes 1179648 | tf_op jit(solution)/shard_map/reduce_scatter | solution.py:37
Sparse Core Ops, SparseCore 0:
  68.8 38.1 all-gather.10
  109.6 81.3 all-gather.8
  194.2 77.8 all-gather.6
  311.2 30.0 reduce-scatter.3
  343.7 96.3 reduce-scatter.5
  442.6 34.6 reduce-scatter.7
where the time goes:
time: 531 us; the launch traced here: 529 us
  waiting for transfers between devices  267 us (50%)
  blocking collectives  147 us (28%)
  local copies, waits for them, and re-layouts  57.9 us (11%)
  matrix products  24.4 us (5%)
  other arithmetic  18 us (3%)
  between operations  14.4 us (3%)
    reduce_scatter x3, waiting for transfers between devices, own_block(): parts = lax.psum_scatter(parts, axes[k], scatter_dimension=0, tiled=True)  166 us
    all_gather x1, waiting for transfers between devices, on_device(): full_tokens = lax.all_gather(tokens, TENSOR, axis=1, tiled=True)  77.7 us
    all_gather x2, blocking collectives, all_blocks(): parts = lax.all_gather(parts, axes[k])  54 us
    all_gather x1, blocking collectives, on_device(): act_full = lax.all_gather(act_cols, TENSOR, axis=1, tiled=True)  53.1 us
    psum x3, blocking collectives, one_axis_at_a_time(): x = lax.psum(x, axis)  40.2 us
    all_gather x1, waiting for transfers between devices, all_blocks(): parts = lax.all_gather(parts, axes[k])  17.5 us
    unnamed x30, local copies, waits for them, and re-layouts  15.8 us
    reshape x1, local copies, waits for them, and re-layouts, own_block(): parts = parts.reshape(*(lax.axis_size(a) for a in axes), *inside)  11.5 us
  transfers between devices with their start and end apart: 6, of which 6 were waited for; matrix products, arithmetic and copies ran while one was open for 9% of the time, Pallas kernels for 0%

commit v1 on v0

--- a/solution.py
+++ b/solution.py
@@ -95,7 +95,9 @@
         normed, proj_first, (((1,), (1,)), ((), ())), preferred_element_type=jnp.float32
     )
     act_cols = jax.nn.gelu(hidden_pre, approximate=False).astype(jnp.bfloat16)
-    act_full = lax.all_gather(act_cols, TENSOR, axis=1, tiled=True)
+    act_full = jnp.concatenate(
+        lax.all_to_all(jnp.stack([act_cols] * lax.axis_size(TENSOR)), TENSOR, 0, 0), axis=1
+    )
     projected = lax.dot_general(
         act_full, proj_second, (((1,), (1,)), ((), ())), preferred_element_type=jnp.float32
     ).astype(jnp.bfloat16)

time: 531 us -> 548 us (1.032)
  waiting for transfers between devices: 267 us -> 321 us
  blocking collectives: 147 us -> 93.8 us
  starting transfers between devices: 0.6 us -> 14.8 us
    all_gather x1 -> x0, blocking collectives: 53.1 us -> none  [on_device(): act_full = lax.all_gather(act_cols, TENSOR, axis=1, tiled=True)]
    all_to_all x0 -> x1, waiting for transfers between devices: none -> 21.1 us  [on_device(): lax.all_to_all(jnp.stack([act_cols] * lax.axis_size(TENSOR)), TENSOR, 0, 0)]
    all_gather x1, waiting for transfers between devices: 17.5 us -> 37.5 us  [all_blocks(): parts = lax.all_gather(parts, axes[k])]
    all_to_all x0 -> x1, starting transfers between devices: none -> 14.4 us  [on_device(): lax.all_to_all(jnp.stack([act_cols] * lax.axis_size(TENSOR)), TENSOR, 0, 0)]
    all_gather x1, waiting for transfers between devices: 5.05 us -> 17 us  [on_device(): lax.all_gather(output_grad, TENSOR, axis=1, tiled=True)]
    unnamed x30 -> x26, local copies, waits for them, and re-layouts: 15.8 us -> 15.8 us
  transfers between devices with their start and end apart: 6 -> 7, of which waited for: 6 -> 7; matrix products, arithmetic and copies ran while one was open for 9% -> 9% of each run, Pallas kernels for 0% -> 0%
where the time goes in v1:
time: 548 us; the launch traced here: 547 us
  waiting for transfers between devices  321 us (59%)
  blocking collectives  93.8 us (17%)
  local copies, waits for them, and re-layouts  59.3 us (11%)
  matrix products  25.6 us (5%)
  other arithmetic  18 us (3%)
  starting transfers between devices  14.8 us (3%)
  between operations  14.4 us (3%)
    reduce_scatter x3, waiting for transfers between devices, own_block(): parts = lax.psum_scatter(parts, axes[k], scatter_dimension=0, tiled=True)  166 us
    all_gather x1, waiting for transfers between devices, on_device(): full_tokens = lax.all_gather(tokens, TENSOR, axis=1, tiled=True)  78.4 us
    all_gather x2, blocking collectives, all_blocks(): parts = lax.all_gather(parts, axes[k])  54 us
    psum x3, blocking collectives, one_axis_at_a_time(): x = lax.psum(x, axis)  39.8 us
    all_gather x1, waiting for transfers between devices, all_blocks(): parts = lax.all_gather(parts, axes[k])  37.5 us
    all_to_all x1, waiting for transfers between devices, on_device(): lax.all_to_all(jnp.stack([act_cols] * lax.axis_size(TENSOR)), TENSOR, 0, 0)  21.1 us
    all_gather x1, waiting for transfers between devices, on_device(): lax.all_gather(output_grad, TENSOR, axis=1, tiled=True)  17 us
    unnamed x26, local copies, waits for them, and re-layouts  15.8 us
  transfers between devices with their start and end apart: 7, of which 7 were waited for; matrix products, arithmetic and copies ran while one was open for 9% of the time, Pallas kernels for 0%

profile of v1, /device:TPU:513, one launch (start us, length us, event | category | flops | bytes accessed | tf_op | source)
XLA Modules:
  0.0 546.8 jit_solution(17470224346475255569)
XLA Ops:
  7.2 0.0 copy-start
  7.2 0.1 all-gather.11.cloned.1.call-start
  7.3 1.4 fusion.34
  8.6 2.0 compare_select_fusion.3
  10.6 2.5 sort.17
  13.1 0.9 copy.42
  14.0 0.7 gather_fusion.2
  14.6 21.0 %all-gather = bf16[640,100]{1,0:T(8,128)(2,1)S(1)} all-gather(bf16[80,100]{1,0:T(8,128)(2,1)S(1)} %gather_fusion.2), channel_id=2, replica_groups=mesh['groups'=2,'tensor_0'=8,'tensor_1'=8,'tensor_2'=2] {'tensor_0'}, dimensions={0}, use_global_device_ids=true | all-gather | bytes 144000 | tf_op jit(solution)/shard_map/all_gather | solution.py:21
  35.6 33.0 %all-gather.1 = bf16[64,80,100]{2,1,0:T(8,128)(2,1)} all-gather(bf16[8,80,100]{2,1,0:T(8,128)(2,1)S(1)} %bitcast.54), channel_id=3, replica_groups=mesh['groups'=2,'tensor_0'=8,'tensor_1'=8,'tensor_2'=2] {'tensor_1'}, dimensions={0}, use_global_device_ids=true | all-gather | bytes 1152000 | tf_op jit(solution)/shard_map/all_gather | solution.py:21
  68.6 0.1 all-gather.11.cloned.1.call-update
  68.7 0.1 all-gather.9.cloned.1.call-start
  68.8 0.7 all-gather.9.cloned.1.call-update
  69.5 37.5 %all-gather.11.cloned.1.call-done = bf16[16,8,80,100]{3,2,1,0:T(8,128)(2,1)} async-done(((bf16[8,8,80,100]{3,2,1,0:T(8,128)(2,1)}), bf16[16,8,80,100]{3,2,1,0:T(8,128)(2,1)}) %all-gather.11.cloned.1.call-update) | async-done | bytes 2048016 | tf_op jit(solution)/shard_map/all_gather | solution.py:21
  107.0 2.3 convert_element_type.79
  109.3 0.8 copy.43
  110.1 2.3 copy-done.2
  112.4 3.9 copy.44
  116.3 6.8 %reshape.117 = f32[80,12800]{1,0:T(8,128)} reshape(f32[80,128,100]{2,1,0:T(8,128)} %copy.44) | data formatting | bytes 8192000 | tf_op jit(solution)/shard_map/convert_element_type | solution.py:58
  123.1 2.5 convert_reduce_fusion
  125.7 0.0 copy-start.9
  125.7 3.5 fusion.4
  129.2 0.1 copy-done.4
  129.4 1.0 fusion.21
  130.4 1.4 stack.2
  131.8 14.4 %all-to-all-start = ((bf16[128,80,48]{1,2,0:T(8,128)(2,1)}), bf16[128,80,48]{1,2,0:T(8,128)(2,1)S(1)}, u32[]{:S(2)}, u32[]{:S(2)}) async-start(bf16[128,80,48]{1,2,0:T(8,128)(2,1)} %stack.2), calls=%async_computation | async-start | bytes 3145728 | tf_op jit(solution)/shard_map/all_to_all | solution.py:99
  146.2 0.1 all-gather.7.cloned.1.call-start
  146.3 1.2 gather_fusion.1
  147.6 11.6 %copy.41 = bf16[48,49152]{0,1:T(8,128)(2,1)} copy(bf16[48,49152]{1,0:T(8,128)(2,1)} %param.24) | data formatting | bytes 9437184 | tf_op args[8]
  159.2 6.9 %gather_fusion = bf16[256,48]{1,0:T(8,128)(2,1)S(1)} fusion(bf16[48,49152]{0,1:T(8,128)(2,1)} %copy.41, s32[1024]{0:T(1024)S(1)} %pad_clamp_fusion.2), kind=kCustom, calls=%fused_computation | custom fusion | bytes 50176 | tf_op jit(solution)/shard_map/jit(_take)/gather | solution.py:105
  166.2 0.1 broadcast_select_fusion
  166.3 21.1 %all-to-all-done = bf16[128,80,48]{1,2,0:T(8,128)(2,1)S(1)} async-done(((bf16[128,80,48]{1,2,0:T(8,128)(2,1)}), bf16[128,80,48]{1,2,0:T(8,128)(2,1)S(1)}, u32[]{:S(2)}, u32[]{:S(2)}) %all-to-all-start) | async-done | bytes 983072 | tf_op jit(solution)/shard_map/all_to_all | solution.py:99
  187.3 1.5 convolution_convert_fusion
  188.8 0.1 copy.45
  188.9 0.9 scatter_fusion
  189.8 0.7 copy.46
  190.5 0.1 all-gather.7.cloned.1.call-update
  190.6 0.1 reduce-scatter.4.cloned.1.call-start
  190.6 17.0 %all-gather.9.cloned.1.call-done = bf16[256,6144]{0,1:T(8,128)(2,1)} async-done(((bf16[256,48]{0,1:T(8,128)(2,1)}), bf16[256,6144]{0,1:T(8,128)(2,1)}) %all-gather.9.cloned.1.call-update) | async-done | bytes 3145744 | tf_op jit(solution)/shard_map/all_gather | solution.py:114
  207.6 3.4 fusion.35
  211.0 78.4 %all-gather.7.cloned.1.call-done = bf16[256,6144]{0,1:T(8,128)(2,1)} async-done(((bf16[256,48]{0,1:T(8,128)(2,1)}), bf16[256,6144]{0,1:T(8,128)(2,1)}) %all-gather.7.cloned.1.call-update) | async-done | bytes 3145744 | tf_op jit(solution)/shard_map/all_gather | solution.py:107
  289.3 2.9 fusion
  292.2 3.5 fusion.10
  295.7 8.0 %fusion.9 = f32[256,6144]{1,0:T(8,128)} fusion(bf16[6144,128]{1,0:T(8,128)(2,1)} %param.26, f32[256,128]{1,0:T(8,128)S(1)} %fusion.35, bf16[6144,128]{1,0:T(8,128)(2,1)S(1)} %copy-done, bf16[256,6144]{0,1:T(8,128)(2,1)} %all-gather.7.cloned.1.call-done, f32[6144]{0:T(1024)S(1)} %copy-done.6, f32[256]{0:T(256)S(1)} %add_rsqrt_fusion, f32[256,128]{1,0:T(8,128)S(1)} %fusion.10), kind=kOutput, calls=%fused_computation.21 | convolution fusion | flops 811925504 | bytes 12870656 | tf_op jit(solution)/shard_map/dot_general | solution.py:124
  303.8 6.4 %convolution_add_fusion = f32[256,6144]{1,0:T(8,128)} fusion(f32[256,6144]{1,0:T(8,128)} %fusion.9, bf16[6144,128]{1,0:T(8,128)(2,1)S(1)} %copy-done, f32[256,128]{1,0:T(8,128)S(1)} %fusion.35, f32[256,128]{1,0:T(8,128)S(1)} %fusion.10), kind=kOutput, calls=%fused_computation.5 | convolution fusion | flops 404422656 | bytes 14417920 | tf_op jit(solution)/shard_map/dot_general | solution.py:127
  310.2 6.6 %copy.47 = f32[256,6144]{0,1:T(8,128)} copy(f32[256,6144]{1,0:T(8,128)} %convolution_add_fusion) | data formatting | bytes 12582912 | tf_op jit(solution)/shard_map/add | solution.py:127
  316.8 11.5 %copy.48 = f32[8,8,2,256,48]{4,3,1,0,2:T(8,128)} copy(f32[8,8,2,256,48]{3,4,2,1,0:T(8,128)} %bitcast.49) | data formatting | bytes 12582912 | tf_op jit(solution)/shard_map/reshape | solution.py:34
  328.4 0.1 reduce-scatter.4.cloned.1.call-update
  328.4 0.1 reduce-scatter.6.cloned.1.call-start
  328.5 30.1 %reduce-scatter.4.cloned.1.call-done = f32[64,256,48]{2,1,0:T(8,128)} async-done(((f32[128,256,48]{2,1,0:T(8,128)}), f32[64,256,48]{2,1,0:T(8,128)}) %reduce-scatter.4.cloned.1.call-update) | async-done | bytes 3145744 | tf_op jit(solution)/shard_map/reduce_scatter | solution.py:37
  358.6 0.1 reduce-scatter.6.cloned.1.call-update
  358.7 0.1 reduce-scatter.8.cloned.1.call-start
  358.8 98.7 %reduce-scatter.6.cloned.1.call-done = f32[8,256,48]{2,1,0:T(8,128)} async-done(((f32[64,256,48]{2,1,0:T(8,128)}), f32[8,256,48]{2,1,0:T(8,128)}) %reduce-scatter.6.cloned.1.call-update) | async-done | bytes 393232 | tf_op jit(solution)/shard_map/reduce_scatter | solution.py:37
  457.5 0.1 reduce-scatter.8.cloned.1.call-update
  457.5 0.1 copy.40
  457.7 0.1 dynamic_slice.3
  457.7 37.2 %reduce-scatter.8.cloned.1.call-done = f32[1,256,48]{2,1,0:T(8,128)} async-done(((f32[8,256,48]{2,1,0:T(8,128)}), f32[1,256,48]{2,1,0:T(8,128)}) %reduce-scatter.8.cloned.1.call-update) | async-done | bytes 49168 | tf_op jit(solution)/shard_map/reduce_scatter | solution.py:37
  495.0 1.1 multiply_reduce_fusion
  496.1 12.7 %psum.21 = f32[256]{0:T(256)S(1)} all-reduce(f32[256]{0:T(256)S(1)} %multiply_reduce_fusion), channel_id=1, replica_groups=mesh['groups'=2,'tensor_0'=8,'tensor_1'=8,'tensor_2'=2] {'tensor_0'}, use_global_device_ids=true, to_apply=%region_9.10 | all-reduce | flops 256 | bytes 2048 | tf_op jit(solution)/shard_map/psum | solution.py:53
  508.8 12.4 %psum.22 = f32[256]{0:T(256)S(1)} all-reduce(f32[256]{0:T(256)S(1)} %psum.21), channel_id=1, replica_groups=mesh['groups'=2,'tensor_0'=8,'tensor_1'=8,'tensor_2'=2] {'tensor_1'}, use_global_device_ids=true, to_apply=%region_10.11 | all-reduce | flops 256 | bytes 2048 | tf_op jit(solution)/shard_map/psum | solution.py:53
  521.1 14.7 %psum.23 = f32[256]{0:T(256)S(1)} all-reduce(f32[256]{0:T(256)S(1)} %psum.22), channel_id=1, replica_groups=mesh['groups'=2,'tensor_0'=8,'tensor_1'=8,'tensor_2'=2] {'tensor_2'}, use_global_device_ids=true, to_apply=%region_11.12 | all-reduce | flops 256 | bytes 2048 | tf_op jit(solution)/shard_map/psum | solution.py:53
  535.9 1.0 multiply_add_fusion
  536.9 0.7 copy.49
  537.6 0.6 gather_fusion.3
  538.2 1.7 fusion.36
  (30 shorter events, 0.1 us)
Async XLA Ops:
  7.2 288.6 %copy-start = (bf16[6144,128]{1,0:T(8,128)(2,1)S(1)}, bf16[6144,128]{1,0:T(8,128)(2,1)}, u32[]{:S(2)}) copy-start(bf16[6144,128]{1,0:T(8,128)(2,1)} %param.27) | copy-start | bytes 4718596
  7.2 99.8 %all-gather.11.cloned.1.call-start = ((), (), s32[]{:S(2)}) async-start(), calls=%async_computation.9 | async-start | bytes 3932160 | tf_op jit(solution)/shard_map/all_gather | solution.py:21
  68.7 138.9 %all-gather.9.cloned.1.call-start = ((), (), s32[]{:S(2)}) async-start(), calls=%async_computation.5 | async-start | bytes 3170304 | tf_op jit(solution)/shard_map/all_gather | solution.py:114
  110.1 2.3 copy-start.2
  123.1 6.1 %copy-start.8 = (bf16[48,12800]{1,0:T(8,128)(2,1)S(1)}, bf16[48,12800]{1,0:T(8,128)(2,1)}, u32[]{:S(2)}) copy-start(bf16[48,12800]{1,0:T(8,128)(2,1)} %param.22) | copy-start | bytes 3686404
  125.6 3.7 copy-start.4
  125.7 3.7 copy-start.9
  125.7 3.7 copy-start.10
  130.4 15.9 %copy-start.1 = (s32[128]{0:T(128)S(1)}, s32[128]{0:T(128)}, u32[]{:S(2)}) copy-start(s32[128]{0:T(128)} %param.18) | copy-start | bytes 1540
  131.8 55.5 %all-to-all-start = ((bf16[128,80,48]{1,2,0:T(8,128)(2,1)}), bf16[128,80,48]{1,2,0:T(8,128)(2,1)S(1)}, u32[]{:S(2)}, u32[]{:S(2)}) async-start(bf16[128,80,48]{1,2,0:T(8,128)(2,1)} %stack.2), calls=%async_computation | async-start | bytes 3145728 | tf_op jit(solution)/shard_map/all_to_all | solution.py:99
  146.2 143.1 %all-gather.7.cloned.1.call-start = ((), (), s32[]{:S(2)}) async-start(), calls=%async_computation.4 | async-start | bytes 3170304 | tf_op jit(solution)/shard_map/all_gather | solution.py:107
  147.6 11.6 %copy-start.7 = (s32[256]{0:T(256)S(1)}, s32[256]{0:T(256)}, u32[]{:S(2)}) copy-start(s32[256]{0:T(256)} %param.19) | copy-start | bytes 3076
  190.6 101.7 %copy-start.6 = (f32[6144]{0:T(1024)S(1)}, f32[6144]{0:T(1024)}, u32[]{:S(2)}) copy-start(f32[6144]{0:T(1024)} %param.25) | copy-start | bytes 73732
  190.6 168.1 %reduce-scatter.4.cloned.1.call-start = ((), (), s32[]{:S(2)}) async-start(), calls=%async_computation.6 | async-start | bytes 25165824 | tf_op jit(solution)/shard_map/reduce_scatter | solution.py:37
  289.3 2.9 copy-start.3
  328.4 129.0 %reduce-scatter.6.cloned.1.call-start = ((), (), s32[]{:S(2)}) async-start(), calls=%async_computation.7 | async-start | bytes 9437184 | tf_op jit(solution)/shard_map/reduce_scatter | solution.py:37
  358.6 98.9 %copy-start.5 = (bf16[256,48]{0,1:T(8,128)(2,1)S(1)}, bf16[256,48]{0,1:T(8,128)(2,1)}, u32[]{:S(2)}) copy-start(bf16[256,48]{0,1:T(8,128)(2,1)} %param.29) | copy-start | bytes 73732
  358.7 136.3 %reduce-scatter.8.cloned.1.call-start = ((), (), s32[]{:S(2)}) async-start(), calls=%async_computation.8 | async-start | bytes 1179648 | tf_op jit(solution)/shard_map/reduce_scatter | solution.py:37
Sparse Core Ops, SparseCore 0:
  68.8 38.1 all-gather.10
  109.6 97.9 all-gather.8
  210.8 78.5 all-gather.6
  328.5 30.0 reduce-scatter.3
  361.0 96.3 reduce-scatter.5
  459.9 35.0 reduce-scatter.7
